TPU v7x, 256 devices: a 4x2x16 block of a 4x16x16 slice. The times are simulated.
256 devices in a mesh: groups: 2 (over y), ctx: 16 (over z), fsdp: 8 (over x, core).
Axes of the slice: x: 4, y: 2, z: 16, core: 2. Of those that a mesh axis runs over, the one named last changes fastest.
The devices are a block of a 4x16x16 slice.
Arguments:
- patches: bfloat16 [16, 4096, 1024], P(('groups', 'fsdp'), 'ctx'), parts along dimension 0, may hold values from -6 to 6
- segment_ids: int32 [16, 4096], P(('groups', 'fsdp'), 'ctx'), parts along dimension 0, may hold values from 0 to 15, never falling along the last dimension, each value on 1 to 3072 neighbouring positions
- patch_rows: int32 [16, 4096], P(('groups', 'fsdp'), 'ctx'), parts along dimension 0, may hold values from 0 to 63
- patch_cols: int32 [16, 4096], P(('groups', 'fsdp'), 'ctx'), parts along dimension 0, may hold values from 0 to 63
- row_table: bfloat16 [64, 1024], replicated, may hold values from -3 to 3
- col_table: bfloat16 [64, 1024], replicated, may hold values from -3 to 3
- norm_gain: float32 [1024], replicated, may hold values from 0.1 to 1.9
- qkv_weight: bfloat16 [1024, 3072], P('fsdp'), may hold values from -5 to 5
- out_weight: bfloat16 [1024, 1024], P(None, 'fsdp'), may hold values from -0.1875 to 0.1875
Outputs:
- encoded: bfloat16 [16, 4096, 1024], P(('groups', 'fsdp'), 'ctx'), parts along dimension 0
There are 2 independent parts, one for each index of `groups`. A program takes and returns all parts, laid end to end along the dimension named above; an argument that names none is the same for every part. Nothing has to cross between parts.
All inputs are finite; a program needn't handle non-finite values.
Results may differ from a plain program's by a relative error of at most 0.0044.
The roundings to bfloat16 on the way count: a program that leaves them out, or rounds other values in their place, can miss the bound.
Values may be sent and summed in bfloat16 or wider, within the bound.
A program may use at most 64 MiB of HBM per device.

v0:
```python
import jax
import jax.numpy as jnp
from jax import lax
from jax.sharding import Mesh
from jax.sharding import PartitionSpec as P

HEADS = 16
FSDP = ("fsdp_0", "fsdp_1")
GROUPS_FSDP = ("groups", "fsdp_0", "fsdp_1")


floor_score = -1e30
epsilon = 1e-06


def laid_out(blocks, dim):
    lengths = list(blocks.shape[1:])
    lengths[dim] *= blocks.shape[0]
    return jnp.moveaxis(blocks, 0, dim).reshape(lengths)


def sent_to_all(value, axis):
    copies = jnp.broadcast_to(value, (lax.axis_size(axis), *value.shape))
    return lax.all_to_all(copies, axis, split_axis=0, concat_axis=0, tiled=True)


def collect(value, axis, dim):
    return laid_out(sent_to_all(value, axis), dim)


def edges_of(length, count):
    unit = 8 if length >= 8 * count else 1
    return [length // unit * k // count * unit for k in range(1, count)]


def stacked_from(value, axes, order):
    blocks = value[None]
    for k in order:
        blocks = lax.all_gather(blocks, axes[k], axis=0, tiled=True)
    block = [lax.axis_size(axes[k]) for k in reversed(order)]
    blocks = blocks.reshape(*block, *value.shape)
    turned = sorted(range(len(order)), key=lambda place: order[len(order) - 1 - place])
    return blocks.transpose(*turned, *range(len(order), blocks.ndim)).reshape(-1, *value.shape)


def spread_gather(value, axes, dim):
    cut = max(range(max(1, value.ndim - 1)), key=lambda d: value.shape[d])
    count, done = (len(axes), [])
    for initial, section in enumerate(
        jnp.split(value, edges_of(value.shape[cut], count), axis=cut)
    ):
        if section.size:
            order = [(initial - k) % count for k in range(count)]
            done.append(stacked_from(section, axes, order))
    return laid_out(jnp.concatenate(done, axis=cut + 1), dim)


def body(
    patches,
    segment_ids,
    patch_rows,
    patch_cols,
    row_table,
    col_table,
    norm_gain,
    qkv_weight,
    out_weight,
):
    tokens = patches[0]
    labels = segment_ids[0]
    model_width = tokens.shape[1]
    head_count = HEADS
    head_size = model_width // head_count
    score_scale = 1.0 / head_size**0.5
    grid_size = row_table.shape[0]
    levels = lax.broadcasted_iota(jnp.int32, (1, grid_size), 1)
    row_onehot = (patch_rows[0][:, None] == levels).astype(jnp.bfloat16)
    col_onehot = (patch_cols[0][:, None] == levels).astype(jnp.bfloat16)
    embedded = (
        tokens.astype(jnp.float32)
        + jnp.dot(row_onehot, row_table, preferred_element_type=jnp.float32)
        + jnp.dot(col_onehot, col_table, preferred_element_type=jnp.float32)
    )
    average = jnp.mean(embedded, axis=-1, keepdims=True)
    centered = embedded - average
    variance = jnp.mean(centered * centered, axis=-1, keepdims=True)
    normed = (centered * lax.rsqrt(variance + epsilon) * norm_gain).astype(jnp.bfloat16)
    qkv = jnp.dot(
        normed,
        lax.all_gather(qkv_weight, FSDP, axis=0, tiled=True),
        preferred_element_type=jnp.float32,
    ).astype(jnp.bfloat16)
    queries = qkv[:, :model_width]
    key_rows = qkv[:, model_width : 2 * model_width]
    value_rows = qkv[:, 2 * model_width :]
    query_part, key_part, value_part = (
        lax.all_to_all(queries, "ctx", split_axis=1, concat_axis=0, tiled=True),
        lax.all_to_all(key_rows, "ctx", split_axis=1, concat_axis=0, tiled=True),
        lax.all_to_all(value_rows, "ctx", split_axis=1, concat_axis=0, tiled=True),
    )
    full_labels = collect(labels, "ctx", 0)
    full_length = query_part.shape[0]
    local_width = query_part.shape[1]
    local_heads = local_width // head_size
    span = min(512, full_length)
    key_heads = key_part.reshape(full_length, local_heads, head_size)
    value_heads = value_part.reshape(full_length, local_heads, head_size)

    def attend_span(offset):
        span_rows = lax.dynamic_slice_in_dim(query_part, offset, span, 0).reshape(
            span, local_heads, head_size
        )
        span_labels = lax.dynamic_slice_in_dim(full_labels, offset, span, 0)
        scores = (
            jnp.einsum("qhd,khd->hqk", span_rows, key_heads, preferred_element_type=jnp.float32)
            * score_scale
        )
        same_segment = (span_labels[:, None] == full_labels[None, :])[None]
        masked = jnp.where(same_segment, scores, floor_score)
        highest = jnp.max(masked, axis=-1, keepdims=True)
        raised = jnp.where(same_segment, jnp.exp(masked - highest), 0.0)
        row_sums = jnp.sum(raised, axis=-1)
        mixed = jnp.einsum(
            "hqk,khd->qhd",
            raised.astype(jnp.bfloat16),
            value_heads,
            preferred_element_type=jnp.float32,
        )
        mixed = mixed / row_sums.T[:, :, None]
        return mixed.reshape(span, local_width).astype(jnp.bfloat16)

    offsets = jnp.arange(full_length // span, dtype=jnp.int32) * span
    head_context = lax.map(attend_span, offsets).reshape(full_length, local_width)
    context = lax.all_to_all(head_context, "ctx", split_axis=0, concat_axis=1, tiled=True)
    attended = jnp.dot(
        context, spread_gather(out_weight, FSDP, 1), preferred_element_type=jnp.float32
    )
    encoded = (embedded + attended).astype(jnp.bfloat16)
    return encoded[None]


def solution(mesh):
    finer = Mesh(
        mesh.devices.reshape(mesh.shape["groups"], mesh.shape["ctx"], 4, 2),
        ("groups", "ctx", "fsdp_0", "fsdp_1"),
    )
    placed = (
        P(GROUPS_FSDP, "ctx", None),
        P(GROUPS_FSDP, "ctx"),
        P(GROUPS_FSDP, "ctx"),
        P(GROUPS_FSDP, "ctx"),
        P(),
        P(),
        P(),
        P(FSDP, None),
        P(None, FSDP),
    )
    return jax.shard_map(
        body, mesh=finer, in_specs=placed, out_specs=P(GROUPS_FSDP, "ctx", None), check_vma=False
    )
```

profile of v0, /device:TPU:33, one launch (start us, length us, event | category | flops | bytes accessed | tf_op | source)
XLA Modules:
  0.0 326.0 jit_solution(15467032216599425548)
XLA Ops:
  7.4 0.7 all-gather.6.cloned.1.call-update
  8.2 1.3 broadcast_in_dim.31
  9.5 24.5 %all-to-all-start = ((s32[16,1,256]{2,1,0:T(1,128)}), s32[16,1,256]{2,1,0:T(1,128)S(1)}, u32[]{:S(2)}, u32[]{:S(2)}) async-start(s32[16,1,256]{2,1,0:T(1,128)} %broadcast_in_dim.31), calls=%async_computation | async-start | bytes 32768 | tf_op jit(solution)/shard_map/all_to_all | solution.py:24
  34.0 1.5 convolution_add_fusion.1
  35.5 1.1 fusion.37
  36.6 0.3 multiply_reduce_fusion
  36.8 35.2 %all-gather.6.cloned.1.call-done = bf16[1024,3072]{1,0:T(8,128)(2,1)} async-done(((bf16[128,3072]{1,0:T(8,128)(2,1)}), bf16[1024,3072]{1,0:T(8,128)(2,1)}) %all-gather.6.cloned.1.call-update) | async-done | bytes 6291472 | tf_op jit(solution)/shard_map/all_gather | solution.py:90
  72.0 4.7 %convolution_convert_fusion = bf16[256,3072]{1,0:T(8,128)(2,1)S(1)} fusion(bf16[1024,3072]{1,0:T(8,128)(2,1)} %all-gather.6.cloned.1.call-done, f32[256,1024]{1,0:T(8,128)S(1)} %get-tuple-element.96, f32[1024]{0:T(1024)} %param.17, f32[256]{0:T(256)S(1)} %add_rsqrt_fusion, f32[256]{0:T(256)S(1)} %broadcast_multiply_fusion), kind=kOutput, calls=%fused_computation.19 | convolution fusion | flops 1612447744 | bytes 8919040 | tf_op jit(solution)/shard_map/dot_general | solution.py:88
  76.8 1.0 copy.42
  77.9 12.1 %all-to-all-start.1 = ((bf16[256,16,64]{0,2,1:T(8,128)(2,1)}), bf16[256,16,64]{0,2,1:T(8,128)(2,1)S(1)}, u32[]{:S(2)}, u32[]{:S(2)}) async-start(bf16[256,16,64]{0,2,1:T(8,128)(2,1)} %bitcast.12), calls=%async_computation.1 | async-start | bytes 1048576 | tf_op jit(solution)/shard_map/all_to_all | solution.py:97
  89.9 1.0 copy.44
  90.9 21.4 %all-to-all-done.1 = bf16[256,16,64]{0,2,1:T(8,128)(2,1)S(1)} async-done(((bf16[256,16,64]{0,2,1:T(8,128)(2,1)}), bf16[256,16,64]{0,2,1:T(8,128)(2,1)S(1)}, u32[]{:S(2)}, u32[]{:S(2)}) %all-to-all-start.1) | async-done | bytes 524320 | tf_op jit(solution)/shard_map/all_to_all | solution.py:97
  112.4 13.1 %all-to-all-start.2 = ((bf16[256,16,64]{0,2,1:T(8,128)(2,1)}), bf16[256,16,64]{0,2,1:T(8,128)(2,1)S(1)}, u32[]{:S(2)}, u32[]{:S(2)}) async-start(bf16[256,16,64]{0,2,1:T(8,128)(2,1)} %bitcast.15), calls=%async_computation.2 | async-start | bytes 1048576 | tf_op jit(solution)/shard_map/all_to_all | solution.py:98
  125.5 1.0 copy.46
  126.5 21.7 %all-to-all-done.2 = bf16[256,16,64]{0,2,1:T(8,128)(2,1)S(1)} async-done(((bf16[256,16,64]{0,2,1:T(8,128)(2,1)}), bf16[256,16,64]{0,2,1:T(8,128)(2,1)S(1)}, u32[]{:S(2)}, u32[]{:S(2)}) %all-to-all-start.2) | async-done | bytes 524320 | tf_op jit(solution)/shard_map/all_to_all | solution.py:98
  148.3 12.8 %all-to-all-start.3 = ((bf16[256,16,64]{0,2,1:T(8,128)(2,1)}), bf16[256,16,64]{0,2,1:T(8,128)(2,1)S(1)}, u32[]{:S(2)}, u32[]{:S(2)}) async-start(bf16[256,16,64]{0,2,1:T(8,128)(2,1)} %bitcast.17), calls=%async_computation.3 | async-start | bytes 1048576 | tf_op jit(solution)/shard_map/all_to_all | solution.py:99
  161.2 10.9 %all-gather = bf16[2048,128]{1,0:T(8,128)(2,1)} all-gather(bf16[512,128]{1,0:T(8,128)(2,1)S(1)} %get-tuple-element.93), channel_id=2, replica_groups=mesh['groups'=2,'ctx'=16,'fsdp_0'=4,'fsdp_1'=2] {'fsdp_0'}, dimensions={0}, use_global_device_ids=true | all-gather | bytes 655360 | tf_op jit(solution)/shard_map/all_gather | solution.py:39
  172.2 1.3 copy.53
  173.6 0.3 copy.45
  173.8 0.2 reshape.102
  174.1 9.7 %all-to-all-done.3 = bf16[256,16,64]{0,2,1:T(8,128)(2,1)S(1)} async-done(((bf16[256,16,64]{0,2,1:T(8,128)(2,1)}), bf16[256,16,64]{0,2,1:T(8,128)(2,1)S(1)}, u32[]{:S(2)}, u32[]{:S(2)}) %all-to-all-start.3) | async-done | bytes 524320 | tf_op jit(solution)/shard_map/all_to_all | solution.py:99
  183.8 0.3 copy.47
  184.4 81.4 %while.10 = (s32[]{:T(128)}, bf16[8,512,64]{1,2,0:T(8,128)(2,1)S(1)}, s32[8]{0:T(128)S(1)}, s32[4096]{0:T(1024)S(1)}, s32[16,256]{1,0:T(8,128)S(1)}, /*index=5*/...) while((s32[]{:T(128)}, ...), condition=%wide.region_5.6_spmd, body=%wide.region_2.5_spmd.sunk | while | flops 570489856 | bytes 26513576 | solution.py:133
  184.4 0.6 dynamic_slice.18
  187.0 2.4 fusion.50
  189.5 2.6 fusion.51
  192.0 2.5 fusion.52
  194.6 0.6 dynamic_slice.18
  197.2 2.4 fusion.50
  199.6 2.6 fusion.51
  202.2 2.5 fusion.52
  204.7 0.6 dynamic_slice.18
  207.4 2.4 fusion.50
  209.8 2.6 fusion.51
  212.4 2.5 fusion.52
  214.9 0.6 dynamic_slice.18
  217.5 2.4 fusion.50
  220.0 2.6 fusion.51
  222.6 2.5 fusion.52
  225.1 0.6 dynamic_slice.18
  227.7 2.4 fusion.50
  230.1 2.6 fusion.51
  232.7 2.5 fusion.52
  235.3 0.6 dynamic_slice.18
  237.9 2.4 fusion.50
  240.3 2.6 fusion.51
  242.9 2.5 fusion.52
  245.4 0.6 dynamic_slice.18
  248.1 2.4 fusion.50
  250.5 2.6 fusion.51
  253.1 2.5 fusion.52
  255.6 0.6 dynamic_slice.18
  258.2 2.4 fusion.50
  260.7 2.6 fusion.51
  263.3 2.5 fusion.52
  265.8 0.3 copy.49
  266.3 1.0 copy.50
  267.2 12.9 %all-to-all-start.4 = ((bf16[16,256,64]{1,2,0:T(8,128)(2,1)}), bf16[16,256,64]{1,2,0:T(8,128)(2,1)}, u32[]{:S(2)}, u32[]{:S(2)}) async-start(bf16[16,256,64]{1,2,0:T(8,128)(2,1)} %copy.50), calls=%async_computation.4 | async-start | bytes 1048576 | tf_op jit(solution)/shard_map/all_to_all | solution.py:134
  280.2 2.6 all-gather.1
  282.9 1.3 copy.51
  284.2 26.2 %all-gather.10.cloned.1.call-done = bf16[8,512,128]{2,1,0:T(8,128)(2,1)} async-done(((bf16[2,512,128]{2,1,0:T(8,128)(2,1)}), bf16[8,512,128]{2,1,0:T(8,128)(2,1)}) %all-gather.10.cloned.1.call-update) | async-done | bytes 1048592 | tf_op jit(solution)/shard_map/all_gather | solution.py:39
  310.4 2.7 maximum_bitcast_fusion
  313.1 2.9 copy.52
  316.0 2.6 fusion.29
  (37 shorter events, 1.6 us)
Async XLA Ops:
  7.4 28.0 %copy-start = (bf16[64,1024]{1,0:T(8,128)(2,1)S(1)}, bf16[64,1024]{1,0:T(8,128)(2,1)}, u32[]{:S(2)}) copy-start(bf16[64,1024]{1,0:T(8,128)(2,1)} %param.16) | copy-start | bytes 393220
  7.4 64.6 %all-gather.6.cloned.1.call-start = ((), (), s32[]{:S(2)}) async-start(), calls=%async_computation.5 | async-start | bytes 7077888 | tf_op jit(solution)/shard_map/all_gather | solution.py:90
  9.5 68.4 %all-to-all-start = ((s32[16,1,256]{2,1,0:T(1,128)}), s32[16,1,256]{2,1,0:T(1,128)S(1)}, u32[]{:S(2)}, u32[]{:S(2)}) async-start(s32[16,1,256]{2,1,0:T(1,128)} %broadcast_in_dim.31), calls=%async_computation | async-start | bytes 32768 | tf_op jit(solution)/shard_map/all_to_all | solution.py:24
  76.7 84.5 %copy-start.1 = (bf16[1024,128]{1,0:T(8,128)(2,1)S(1)}, bf16[1024,128]{1,0:T(8,128)(2,1)}, u32[]{:S(2)}) copy-start(bf16[1024,128]{1,0:T(8,128)(2,1)} %param.19) | copy-start | bytes 786436
  77.9 34.5 %all-to-all-start.1 = ((bf16[256,16,64]{0,2,1:T(8,128)(2,1)}), bf16[256,16,64]{0,2,1:T(8,128)(2,1)S(1)}, u32[]{:S(2)}, u32[]{:S(2)}) async-start(bf16[256,16,64]{0,2,1:T(8,128)(2,1)} %bitcast.12), calls=%async_computation.1 | async-start | bytes 1048576 | tf_op jit(solution)/shard_map/all_to_all | solution.py:97
  112.4 35.9 %all-to-all-start.2 = ((bf16[256,16,64]{0,2,1:T(8,128)(2,1)}), bf16[256,16,64]{0,2,1:T(8,128)(2,1)S(1)}, u32[]{:S(2)}, u32[]{:S(2)}) async-start(bf16[256,16,64]{0,2,1:T(8,128)(2,1)} %bitcast.15), calls=%async_computation.2 | async-start | bytes 1048576 | tf_op jit(solution)/shard_map/all_to_all | solution.py:98
  148.3 35.6 %all-to-all-start.3 = ((bf16[256,16,64]{0,2,1:T(8,128)(2,1)}), bf16[256,16,64]{0,2,1:T(8,128)(2,1)S(1)}, u32[]{:S(2)}, u32[]{:S(2)}) async-start(bf16[256,16,64]{0,2,1:T(8,128)(2,1)} %bitcast.17), calls=%async_computation.3 | async-start | bytes 1048576 | tf_op jit(solution)/shard_map/all_to_all | solution.py:99
  161.1 121.7 %all-gather.8.cloned.1.call-start = ((), (), s32[]{:S(2)}) async-start(), calls=%async_computation.6 | async-start | bytes 1572864 | tf_op jit(solution)/shard_map/all_gather | solution.py:39
  267.2 48.8 %all-to-all-start.4 = ((bf16[16,256,64]{1,2,0:T(8,128)(2,1)}), bf16[16,256,64]{1,2,0:T(8,128)(2,1)}, u32[]{:S(2)}, u32[]{:S(2)}) async-start(bf16[16,256,64]{1,2,0:T(8,128)(2,1)} %copy.50), calls=%async_computation.4 | async-start | bytes 1048576 | tf_op jit(solution)/shard_map/all_to_all | solution.py:134
  280.1 30.3 %all-gather.10.cloned.1.call-start = ((), (), s32[]{:S(2)}) async-start(), calls=%async_computation.7 | async-start | bytes 1310720 | tf_op jit(solution)/shard_map/all_gather | solution.py:39
Sparse Core Ops, SparseCore 0:
  10.1 61.9 all-gather.5
Sparse Core Ops, SparseCore 1:
  172.3 22.0 all-gather.7
  282.9 27.4 all-gather.9
where the time goes:
time: 328 us; the launch traced here: 326 us
  waiting for transfers between devices  115 us (35%)
  starting transfers between devices  75.6 us (23%)
  matrix products  49.4 us (15%)
  other arithmetic  23.6 us (7%)
  local copies, waits for them, and re-layouts  17.8 us (5%)
  loops' own time  15.8 us (5%)
  between operations  15.1 us (5%)
  blocking collectives  13.5 us (4%)
    all_gather x1, waiting for transfers between devices, body(): lax.all_gather(qkv_weight, FSDP, axis=0, tiled=True)  35.2 us
    all_gather x2, waiting for transfers between devices, stacked_from(): blocks = lax.all_gather(blocks, axes[k], axis=0, tiled=True)  26.2 us
    all_to_all x1, starting transfers between devices, sent_to_all(): return lax.all_to_all(copies, axis, split_axis=0, concat_axis=0, tiled=True)  24.5 us
    all_to_all x1, waiting for transfers between devices, body(): lax.all_to_all(key_rows, 'ctx', split_axis=1, concat_axis=0, tiled=True)  21.7 us
    all_to_all x1, waiting for transfers between devices, body(): lax.all_to_all(queries, 'ctx', split_axis=1, concat_axis=0, tiled=True)  21.4 us
    reduce_sum x8, other arithmetic, attend_span(): row_sums = jnp.sum(raised, axis=-1)  20.6 us
    dot_general x8, matrix products, attend_span(): jnp.einsum('hqk,khd->qhd', raised.astype(jnp.bfloat16), value_heads, pref...  20.1 us
    dot_general x8, matrix products, attend_span(): jnp.einsum('qhd,khd->hqk', span_rows, key_heads, preferred_element_type=j...  19.5 us
  transfers between devices with their start and end apart: 8, of which 5 were waited for; matrix products, arithmetic and copies ran while one was open for 27% of the time, Pallas kernels for 0%

commit v1 on v0

v1 whole, which is shorter than its diff:
```python
import functools

import jax
import jax.numpy as jnp
from jax import lax
from jax.experimental import pallas as pl
from jax.experimental.pallas import tpu as pltpu
from jax.sharding import PartitionSpec as P

HEADS = 16
LANES = 128
epsilon = 1e-06
floor_score = -1e30
MESH = pl.DeviceIdType.MESH
F32 = jnp.float32
BF16 = jnp.bfloat16


def flip(value):
    return pltpu.roll(value, LANES // 2, 1)


def far_first(count, step):
    odd = lax.rem(step, 2)
    return count // 2 + (1 - odd) * (step // 2) - odd * ((step + 1) // 2)


def block_kernel(
    ring,
    shards,
    patches,
    labels,
    patch_rows,
    patch_cols,
    row_table,
    col_table,
    gain,
    w_own,
    ow_own,
    out,
    w_all,
    ow_all,
    onehots,
    embedded,
    normed,
    kv_out,
    kv_in,
    q_out,
    q_in,
    c_out,
    c_in,
    labels_in,
    k_aug,
    scores,
    context,
    w_sent,
    w_come,
    ow_sent,
    ow_come,
    kv_sent,
    kv_come,
    q_sent,
    q_come,
    c_sent,
    c_come,
    l_sent,
    l_come,
):
    tokens, width = patches.shape
    half_tokens = tokens // 2
    depth = w_own.shape[0]
    pairs = width // LANES
    chips = shards // 2
    me = lax.axis_index("ctx")
    shard = lax.axis_index("fsdp")
    chip, core = shard // 2, lax.rem(shard, 2)
    own_pair = me // 2
    partner = 2 * chip + 1 - core

    def mate(k, which):
        return 2 * lax.rem(chip + k, chips) + which

    barrier = pltpu.get_barrier_semaphore()
    for k in range(1, chips):
        pl.semaphore_signal(
            barrier, inc=1, device_id={"fsdp": mate(k, core)}, device_id_type=MESH
        )
    pl.semaphore_signal(barrier, inc=1, device_id={"fsdp": partner}, device_id_type=MESH)

    def greet(k, carry):
        pl.semaphore_signal(
            barrier, inc=1, device_id={"ctx": lax.rem(me + k, ring)}, device_id_type=MESH
        )
        return carry

    lax.fori_loop(1, ring, greet, 0)
    pl.semaphore_wait(barrier, ring - 1 + chips)

    lane = lax.broadcasted_iota(jnp.int32, (half_tokens, LANES), 1)
    low = lane < LANES // 2
    lane_full = lax.broadcasted_iota(jnp.int32, (tokens, LANES), 1)
    low_full = lane_full < LANES // 2

    def columns(tile):
        return pl.ds(pl.multiple_of(tile * LANES, LANES), LANES)

    def w_rows(source):
        return pl.ds(pl.multiple_of(source * depth, depth), depth)

    def w_send(tile, target):
        pltpu.make_async_remote_copy(
            src_ref=w_own.at[:, columns(tile)],
            dst_ref=w_all.at[w_rows(shard), columns(tile)],
            send_sem=w_sent.at[tile],
            recv_sem=w_come.at[tile, shard],
            device_id={"fsdp": target},
            device_id_type=MESH,
        ).start()

    def w_wait(tile, source):
        place = w_all.at[w_rows(source), columns(tile)]
        pltpu.make_async_copy(place, place, w_come.at[tile, source]).wait()

    def w_forward(tile, source):
        place = w_all.at[w_rows(source), columns(tile)]
        pltpu.make_async_remote_copy(
            src_ref=place,
            dst_ref=place,
            send_sem=w_sent.at[tile],
            recv_sem=w_come.at[tile, source],
            device_id={"fsdp": partner},
            device_id_type=MESH,
        ).start()

    def pair_of(step):
        return lax.rem(own_pair + far_first(pairs, step), pairs)

    order = [2, 1, 3] if chips == 4 else list(range(1, chips))

    def spread(tiles):
        for k in order:
            for tile in tiles:
                w_send(tile, mate(k, core))
        for tile in tiles:
            w_send(tile, partner)

    def gather(tiles):
        for k in order[1:] + order[:1]:
            for tile in tiles:
                w_wait(tile, mate(k, core))
                w_forward(tile, mate(k, core))
        for tile in tiles:
            w_wait(tile, partner)
        for k in order[1:] + order[:1]:
            for tile in tiles:
                w_wait(tile, mate(k, 1 - core))

    def kv_tiles(step):
        pair = pair_of(step)
        return pairs + pair, 2 * pairs + pair

    def q_tiles(step):
        return (pair_of(step),)

    for step in range(2):
        spread(kv_tiles(step))

    def tell(k, carry):
        target = lax.rem(me + k, ring)
        pltpu.make_async_remote_copy(
            src_ref=labels,
            dst_ref=labels_in.at[me],
            send_sem=l_sent,
            recv_sem=l_come.at[me],
            device_id={"ctx": target},
            device_id_type=MESH,
        ).start()
        return carry

    lax.fori_loop(1, ring, tell, 0)
    labels_in[me] = labels[...]

    levels = lax.broadcasted_iota(jnp.int32, (LANES, tokens), 0)
    grid_size = row_table.shape[0]
    hit = (levels == patch_rows[...]) | (levels == patch_cols[...] + grid_size)
    onehots[...] = jnp.where(hit, 1.0, 0.0).T.astype(BF16)
    table = jnp.concatenate([row_table[...], col_table[...]], axis=0)
    scale = gain[...]
    strip = 64

    def embed(i, carry):
        rows = pl.ds(pl.multiple_of(i * strip, strip), strip)
        value = patches[rows, :].astype(F32) + jnp.dot(
            onehots[rows, :], table, preferred_element_type=F32
        )
        embedded[rows, :] = value
        average = jnp.mean(value, axis=-1, keepdims=True)
        centered = value - average
        variance = jnp.mean(centered * centered, axis=-1, keepdims=True)
        normed[rows, :] = (centered * lax.rsqrt(variance + epsilon) * scale).astype(BF16)
        return carry

    lax.fori_loop(0, tokens // strip, embed, 0)
    w_all[w_rows(shard), :] = w_own[...]

    def project(tile):
        return jnp.dot(normed[...], w_all[:, columns(tile)], preferred_element_type=F32)

    def deliver(outgoing, incoming, sent, come, target):
        @pl.when(target != me)
        def _():
            pltpu.make_async_remote_copy(
                src_ref=outgoing.at[target],
                dst_ref=incoming.at[me],
                send_sem=sent,
                recv_sem=come.at[me],
                device_id={"ctx": target},
                device_id_type=MESH,
            ).start()

        @pl.when(target == me)
        def _():
            incoming[me] = outgoing[target]

    def kv_step(step, carry):
        @pl.when(step < pairs - 2)
        def _():
            spread(kv_tiles(step + 2))

        @pl.when(step >= pairs - 2)
        def _():
            spread(q_tiles(step + 2 - pairs))

        k_tile, v_tile = kv_tiles(step)
        gather((k_tile, v_tile))
        keys = project(k_tile)
        values = project(v_tile)
        first = 2 * pair_of(step)
        kv_out[first] = jnp.where(low_full, keys, flip(values)).astype(BF16)
        kv_out[first + 1] = jnp.where(low_full, flip(keys), values).astype(BF16)
        deliver(kv_out, kv_in, kv_sent, kv_come, first)
        deliver(kv_out, kv_in, kv_sent, kv_come, first + 1)
        return carry

    lax.fori_loop(0, pairs, kv_step, 0)

    def ow_place(source):
        return ow_all.at[:, columns(source)]

    def ow_wait(source):
        pltpu.make_async_copy(ow_place(source), ow_place(source), ow_come.at[source]).wait()

    score_scale = 1.0 / (LANES // 2) ** 0.5

    def q_step(step, carry):
        @pl.when(step < pairs - 2)
        def _():
            spread(q_tiles(step + 2))

        @pl.when(step == pairs - 2)
        def _():
            for k in order + [0]:
                pltpu.make_async_remote_copy(
                    src_ref=ow_own,
                    dst_ref=ow_place(shard),
                    send_sem=ow_sent,
                    recv_sem=ow_come.at[shard],
                    device_id={"fsdp": mate(k, core) if k else partner},
                    device_id_type=MESH,
                ).start()

        (tile,) = q_tiles(step)
        gather((tile,))
        queries = project(tile) * score_scale
        upper, lower = queries[:half_tokens], queries[half_tokens:]
        first = 2 * pair_of(step)
        q_out[first] = jnp.where(low, upper, flip(lower)).astype(BF16)
        q_out[first + 1] = jnp.where(low, flip(upper), lower).astype(BF16)
        deliver(q_out, q_in, q_sent, q_come, first)
        deliver(q_out, q_in, q_sent, q_come, first + 1)
        return carry

    lax.fori_loop(0, pairs, q_step, 0)

    for k in order:
        ow_wait(mate(k, core))
        pltpu.make_async_remote_copy(
            src_ref=ow_place(mate(k, core)),
            dst_ref=ow_place(mate(k, core)),
            send_sem=ow_sent,
            recv_sem=ow_come.at[mate(k, core)],
            device_id={"fsdp": partner},
            device_id_type=MESH,
        ).start()
    ow_all[:, columns(shard)] = ow_own[...]

    label_levels = levels - LANES // 2

    def token_rows(source):
        return pl.ds(pl.multiple_of(source * tokens, tokens), tokens)

    def label_hits(source):
        return jnp.where(label_levels == labels_in[source], 1.0, 0.0).T

    def widen(i, carry):
        source = lax.rem(me + far_first(ring, i), ring)

        @pl.when(source != me)
        def _():
            pltpu.make_async_copy(labels, labels_in.at[source], l_come.at[source]).wait()
            pltpu.make_async_copy(
                kv_out.at[source], kv_in.at[source], kv_come.at[source]
            ).wait()

        other = jnp.where(label_hits(source) > 0.5, 0.0, floor_score).astype(BF16)
        k_aug[token_rows(source), :] = jnp.where(low_full, kv_in[source], other)
        return carry

    lax.fori_loop(0, ring, widen, 0)

    span = 512
    spans = ring * tokens // span
    per_span = span // tokens

    def attend(i, carry):
        offset = jnp.where(i == 0, 0, far_first(ring, i - 1))
        source = lax.rem(me + offset, ring)

        @pl.when(i > 0)
        def _():
            pltpu.make_async_copy(q_out.at[source], q_in.at[source], q_come.at[source]).wait()

        block = q_in[source].astype(F32)
        hits = label_hits(source)
        upper = jnp.where(low, block, hits[:half_tokens])
        lower = jnp.where(low, flip(block), hits[half_tokens:])
        queries = jnp.concatenate([upper, lower], axis=0).astype(BF16)
        highest = jnp.full((tokens, LANES), -jnp.inf, F32)
        for j in range(spans):
            part = lax.dot_general(
                queries,
                k_aug[pl.ds(j * span, span), :],
                (((1,), (1,)), ((), ())),
                preferred_element_type=F32,
            )
            scores[:, pl.ds(j * span, span)] = part
            for t in range(span // LANES):
                highest = jnp.maximum(highest, part[:, t * LANES : (t + 1) * LANES])
        top = jnp.max(highest, axis=-1, keepdims=True)
        sums = jnp.zeros((tokens, LANES), F32)
        mixed = jnp.zeros((tokens, LANES), F32)
        for j in range(spans):
            raised = jnp.exp(scores[:, pl.ds(j * span, span)] - top)
            for t in range(span // LANES):
                sums = sums + raised[:, t * LANES : (t + 1) * LANES]
            values = kv_in[pl.ds(j * per_span, per_span)].reshape(span, LANES)
            mixed = mixed + jnp.dot(raised.astype(BF16), values, preferred_element_type=F32)
        mixed = mixed / jnp.sum(sums, axis=-1, keepdims=True)
        packed = jnp.where(low, flip(mixed[:half_tokens]), mixed[half_tokens:])
        c_out[source] = packed.astype(BF16)
        deliver(c_out, c_in, c_sent, c_come, source)
        return carry

    lax.fori_loop(0, ring, attend, 0)

    ow_wait(partner)
    for k in order:
        ow_wait(mate(k, 1 - core))

    def collect(i, carry):
        source = lax.rem(me + far_first(ring, i), ring)

        @pl.when(source != me)
        def _():
            pltpu.make_async_copy(c_out.at[source], c_in.at[source], c_come.at[source]).wait()

        return carry

    lax.fori_loop(0, ring, collect, 0)
    for pair in range(pairs):
        left = c_in[2 * pair].astype(F32)
        right = c_in[2 * pair + 1].astype(F32)
        place = pl.ds(pair * LANES, LANES)
        context[pl.ds(0, half_tokens), place] = jnp.where(low, left, flip(right)).astype(BF16)
        context[pl.ds(half_tokens, half_tokens), place] = jnp.where(
            low, flip(left), right
        ).astype(BF16)
    wide = 256

    def finish(i, carry):
        place = pl.ds(pl.multiple_of(i * wide, wide), wide)
        attended = jnp.dot(context[...], ow_all[:, place], preferred_element_type=F32)
        out[:, place] = (embedded[:, place] + attended).astype(BF16)
        return carry

    lax.fori_loop(0, width // wide, finish, 0)

    def drain(tile, carry):
        place = w_all.at[pl.ds(0, (2 * chips - 1) * depth), columns(tile)]
        pltpu.make_async_copy(place, place, w_sent.at[tile]).wait()
        return carry

    lax.fori_loop(0, 3 * pairs, drain, 0)
    place = ow_all.at[:, pl.ds(0, (2 * chips - 1) * LANES)]
    pltpu.make_async_copy(place, place, ow_sent).wait()
    for buffer, sent in ((kv_out, kv_sent), (q_out, q_sent), (c_out, c_sent), (labels_in, l_sent)):
        place = buffer.at[pl.ds(0, ring - 1)]
        pltpu.make_async_copy(place, place, sent).wait()


def body(
    ring,
    shards,
    patches,
    segment_ids,
    patch_rows,
    patch_cols,
    row_table,
    col_table,
    norm_gain,
    qkv_weight,
    out_weight,
):
    _, tokens, width = patches.shape
    pairs = width // LANES
    dma = pltpu.SemaphoreType.DMA
    result = pl.pallas_call(
        functools.partial(block_kernel, ring, shards),
        out_shape=jax.ShapeDtypeStruct((tokens, width), BF16),
        in_specs=[pl.BlockSpec(memory_space=pltpu.VMEM)] * 9,
        out_specs=pl.BlockSpec(memory_space=pltpu.VMEM),
        scratch_shapes=[
            pltpu.VMEM((width, 3 * width), BF16),
            pltpu.VMEM((width, width), BF16),
            pltpu.VMEM((tokens, LANES), BF16),
            pltpu.VMEM((tokens, width), F32),
            pltpu.VMEM((tokens, width), BF16),
            pltpu.VMEM((ring, tokens, LANES), BF16),
            pltpu.VMEM((ring, tokens, LANES), BF16),
            pltpu.VMEM((ring, tokens // 2, LANES), BF16),
            pltpu.VMEM((ring, tokens // 2, LANES), BF16),
            pltpu.VMEM((ring, tokens // 2, LANES), BF16),
            pltpu.VMEM((ring, tokens // 2, LANES), BF16),
            pltpu.VMEM((ring, 1, tokens), jnp.int32),
            pltpu.VMEM((ring * tokens, LANES), BF16),
            pltpu.VMEM((tokens, ring * tokens), F32),
            pltpu.VMEM((tokens, width), BF16),
            dma((3 * pairs,)),
            dma((3 * pairs, shards)),
            dma,
            dma((shards,)),
            dma,
            dma((ring,)),
            dma,
            dma((ring,)),
            dma,
            dma((ring,)),
            dma,
            dma((ring,)),
        ],
        compiler_params=pltpu.CompilerParams(
            collective_id=0, has_side_effects=True, vmem_limit_bytes=60 << 20
        ),
        name="encoder_block",
    )(
        patches[0],
        segment_ids,
        patch_rows,
        patch_cols,
        row_table,
        col_table,
        norm_gain[None],
        qkv_weight,
        out_weight,
    )
    return result[None]


def solution(mesh):
    ring, shards = mesh.shape["ctx"], mesh.shape["fsdp"]
    tokens_spec = P(("groups", "fsdp"), "ctx")
    placed = (
        P(("groups", "fsdp"), "ctx", None),
        tokens_spec,
        tokens_spec,
        tokens_spec,
        P(),
        P(),
        P(),
        P("fsdp", None),
        P(None, "fsdp"),
    )
    return jax.shard_map(
        functools.partial(body, ring, shards),
        mesh=mesh,
        in_specs=placed,
        out_specs=P(("groups", "fsdp"), "ctx", None),
        check_vma=False,
    )
```

time: 328 us -> 136 us (0.41)
  Pallas kernels: 0 us -> 134 us
  waiting for transfers between devices: 115 us -> 0 us
  starting transfers between devices: 75.6 us -> 0 us
  matrix products: 49.4 us -> 0 us
  other arithmetic: 23.6 us -> 0 us
  local copies, waits for them, and re-layouts: 17.8 us -> 1.87 us
  loops' own time: 15.8 us -> 0 us
  between operations: 15.1 us -> 0.01 us
  blocking collectives: 13.5 us -> 0 us
    pallas_call x0 -> x1, Pallas kernels: none -> 134 us  [body(): pl.pallas_call(functools.partial(block_kernel, ring, shards), out_shape=j...]
    all_to_all x5 -> x0, starting transfers between devices: 75.5 us -> none  [the longest x1 24.5 us: sent_to_all(): return lax.all_to_all(copies, axis, split_axis=0, concat_axis=0, tiled=True)]
    all_gather x3 -> x0, waiting for transfers between devices: 61.4 us -> none  [the longest x1 35.2 us: body(): lax.all_gather(qkv_weight, FSDP, axis=0, tiled=True)]
    all_to_all x5 -> x0, waiting for transfers between devices: 52.9 us -> none  [the longest x1 21.7 us: body(): lax.all_to_all(key_rows, 'ctx', split_axis=1, concat_axis=0, tiled=True)]
    dot_general x20 -> x0, matrix products: 49.4 us -> none  [the longest x8 20.1 us: attend_span(): jnp.einsum('hqk,khd->qhd', raised.astype(jnp.bfloat16), value_heads, pref...]
    reduce_sum x9 -> x0, other arithmetic: 20.9 us -> none  [the longest x8 20.6 us: attend_span(): row_sums = jnp.sum(raised, axis=-1)]
    another operation x1 -> x0, loops' own time: 15.8 us -> none  [body(): lax.map(attend_span, offsets).reshape(full_length, local_width)]
    all_gather x2 -> x0, blocking collectives: 13.5 us -> none  [stacked_from(): blocks = lax.all_gather(blocks, axes[k], axis=0, tiled=True)]
  transfers between devices with their start and end apart: 8 -> 0, of which waited for: 5 -> 0; matrix products, arithmetic and copies ran while one was open for 27% -> 0% of each run, Pallas kernels for 0% -> 0%
where the time goes in v1:
time: 136 us
  Pallas kernels  134 us (99%)
  local copies, waits for them, and re-layouts  1.87 us (1%)
    pallas_call x1, Pallas kernels, body(): pl.pallas_call(functools.partial(block_kernel, ring, shards), out_shape=j...  134 us

profile of v1, /device:TPU:33, one launch (start us, length us, event | category | flops | bytes accessed | tf_op | source)
XLA Modules:
  0.0 135.9 jit_solution(5873968593536150554)
XLA Ops:
  0.0 134.0 %encoder_block.1 = bf16[256,1024]{1,0:T(8,128)(2,1)} custom-call(bf16[256,1024]{1,0:T(8,128)(2,1)} %bitcast.4, s32[1,256]{1,0:T(1,128)} %labels.1, s32[1,256]{1,0:T(1,128)} %patch_rows.1, s32[1,256]{1,0:T(1,128)} %patch_cols.1, bf16[64,1024]{1,0:T(8,128)(2,1)} %row_table.1, bf16[64,1024]{1,0:T(8,128)(2,1)} %col_table.1, f32[1,1024]{1,0:T(1,128)} %bitcast.5, ...), custom_call_target="tpu_custom_call" | custom-call | tf_op jit(solution)/shard_map/encoder_block/pallas_call | solution.py:427
  134.0 1.9 %copy.11 = bf16[1,256,1024]{2,1,0:T(8,128)(2,1)} copy(bf16[1,256,1024]{2,1,0:T(8,128)(2,1)} %bitcast.3) | data formatting | bytes 1048576

commit v2 on v1

--- a/solution.py
+++ b/solution.py
@@ -65,6 +65,8 @@
     c_come,
     l_sent,
     l_come,
+    below_here,
+    here,
 ):
     tokens, width = patches.shape
     half_tokens = tokens // 2
@@ -81,20 +83,25 @@
         return 2 * lax.rem(chip + k, chips) + which
 
     barrier = pltpu.get_barrier_semaphore()
+    has_below, has_above = me > 0, me < ring - 1
+
+    def greet(**where):
+        pl.semaphore_signal(barrier, inc=1, device_id=where, device_id_type=MESH)
+
     for k in range(1, chips):
-        pl.semaphore_signal(
-            barrier, inc=1, device_id={"fsdp": mate(k, core)}, device_id_type=MESH
-        )
-    pl.semaphore_signal(barrier, inc=1, device_id={"fsdp": partner}, device_id_type=MESH)
-
-    def greet(k, carry):
-        pl.semaphore_signal(
-            barrier, inc=1, device_id={"ctx": lax.rem(me + k, ring)}, device_id_type=MESH
-        )
-        return carry
-
-    lax.fori_loop(1, ring, greet, 0)
-    pl.semaphore_wait(barrier, ring - 1 + chips)
+        greet(fsdp=mate(k, core))
+    greet(fsdp=partner)
+
+    @pl.when(has_below)
+    def _():
+        greet(ctx=me - 1)
+
+    @pl.when(has_above)
+    def _():
+        greet(ctx=me + 1)
+
+    neighbours = jnp.where(has_below, 1, 0) + jnp.where(has_above, 1, 0)
+    pl.semaphore_wait(barrier, chips + neighbours)
 
     lane = lax.broadcasted_iota(jnp.int32, (half_tokens, LANES), 1)
     low = lane < LANES // 2
@@ -155,8 +162,11 @@
             for tile in tiles:
                 w_wait(tile, mate(k, 1 - core))
 
+    def rising_pair(step):
+        return jnp.where(step < own_pair, own_pair - 1 - step, step)
+
     def kv_tiles(step):
-        pair = pair_of(step)
+        pair = rising_pair(step)
         return pairs + pair, 2 * pairs + pair
 
     def q_tiles(step):
@@ -165,19 +175,41 @@
     for step in range(2):
         spread(kv_tiles(step))
 
-    def tell(k, carry):
-        target = lax.rem(me + k, ring)
-        pltpu.make_async_remote_copy(
-            src_ref=labels,
-            dst_ref=labels_in.at[me],
-            send_sem=l_sent,
-            recv_sem=l_come.at[me],
-            device_id={"ctx": target},
-            device_id_type=MESH,
-        ).start()
-        return carry
-
-    lax.fori_loop(1, ring, tell, 0)
+    @pl.when(has_below)
+    def _():
+        pl.semaphore_wait(below_here, 1)
+
+    @pl.when(has_above)
+    def _():
+        pl.semaphore_signal(below_here, inc=1, device_id={"ctx": me + 1}, device_id_type=MESH)
+
+    def announce(target, carry):
+        @pl.when(target < me)
+        def _():
+            pl.semaphore_signal(
+                here.at[me], inc=1, device_id={"ctx": target}, device_id_type=MESH
+            )
+
+        return carry
+
+    lax.fori_loop(0, ring, announce, 0)
+
+    def tell_labels(target):
+        @pl.when(target > me)
+        def _():
+            pl.semaphore_wait(here.at[target], 1)
+
+        @pl.when(target != me)
+        def _():
+            pltpu.make_async_remote_copy(
+                src_ref=labels,
+                dst_ref=labels_in.at[me],
+                send_sem=l_sent,
+                recv_sem=l_come.at[me],
+                device_id={"ctx": target},
+                device_id_type=MESH,
+            ).start()
+
     labels_in[me] = labels[...]
 
     levels = lax.broadcasted_iota(jnp.int32, (LANES, tokens), 0)
@@ -235,11 +267,12 @@
         gather((k_tile, v_tile))
         keys = project(k_tile)
         values = project(v_tile)
-        first = 2 * pair_of(step)
+        first = 2 * rising_pair(step)
         kv_out[first] = jnp.where(low_full, keys, flip(values)).astype(BF16)
         kv_out[first + 1] = jnp.where(low_full, flip(keys), values).astype(BF16)
-        deliver(kv_out, kv_in, kv_sent, kv_come, first)
-        deliver(kv_out, kv_in, kv_sent, kv_come, first + 1)
+        for target in (first, first + 1):
+            tell_labels(target)
+            deliver(kv_out, kv_in, kv_sent, kv_come, target)
         return carry
 
     lax.fori_loop(0, pairs, kv_step, 0)
@@ -302,9 +335,7 @@
     def label_hits(source):
         return jnp.where(label_levels == labels_in[source], 1.0, 0.0).T
 
-    def widen(i, carry):
-        source = lax.rem(me + far_first(ring, i), ring)
-
+    def widen(source, carry):
         @pl.when(source != me)
         def _():
             pltpu.make_async_copy(labels, labels_in.at[source], l_come.at[source]).wait()
@@ -323,8 +354,7 @@
     per_span = span // tokens
 
     def attend(i, carry):
-        offset = jnp.where(i == 0, 0, far_first(ring, i - 1))
-        source = lax.rem(me + offset, ring)
+        source = jnp.where(i == 0, me, jnp.where(i <= me, i - 1, i))
 
         @pl.when(i > 0)
         def _():
@@ -457,9 +487,11 @@
             dma((ring,)),
             dma,
             dma((ring,)),
+            pltpu.SemaphoreType.REGULAR,
+            pltpu.SemaphoreType.REGULAR((ring,)),
         ],
         compiler_params=pltpu.CompilerParams(
-            collective_id=0, has_side_effects=True, vmem_limit_bytes=60 << 20
+            collective_id=0, has_side_effects=True, vmem_limit_bytes=36 << 20
         ),
         name="encoder_block",
     )(

time: 136 us -> 151 us (1.11)
  Pallas kernels: 134 us -> 144 us
  local copies, waits for them, and re-layouts: 1.87 us -> 7.12 us
    pallas_call x1, Pallas kernels: 134 us -> 144 us  [body(): pl.pallas_call(functools.partial(block_kernel, ring, shards), out_shape=j...]
    unnamed x1 -> x19, local copies, waits for them, and re-layouts: 1.87 us -> 7.12 us
where the time goes in v2:
time: 151 us
  Pallas kernels  144 us (95%)
  local copies, waits for them, and re-layouts  7.12 us (5%)
    pallas_call x1, Pallas kernels, body(): pl.pallas_call(functools.partial(block_kernel, ring, shards), out_shape=j...  144 us
    unnamed x19, local copies, waits for them, and re-layouts  7.12 us

profile of v2, /device:TPU:33, one launch (start us, length us, event | category | flops | bytes accessed | tf_op | source)
XLA Modules:
  0.0 150.8 jit_solution(12512245989391323903)
XLA Ops:
  0.0 0.0 copy-start.7
  0.0 0.0 copy-start.8
  0.0 0.0 copy-start.6
  0.0 0.7 copy-done.7
  0.7 0.0 copy-done.8
  0.7 0.0 copy-done.6
  0.7 0.0 copy-start
  0.7 1.1 copy-done
  1.8 0.0 copy-start.1
  1.8 1.0 copy-done.1
  2.9 0.0 copy-start.2
  2.9 0.9 copy-done.2
  3.8 0.0 copy-start.3
  3.8 0.9 copy-done.3
  4.7 0.0 copy-start.4
  4.7 0.9 copy-done.4
  5.6 0.0 copy-start.5
  5.6 0.7 copy-done.5
  6.3 143.7 %encoder_block.1 = bf16[256,1024]{1,0:T(8,128)(2,1)S(1)} custom-call(bf16[256,1024]{1,0:T(8,128)(2,1)S(1)} %bitcast.4, s32[1,256]{1,0:T(1,128)S(1)} %copy-done.6, s32[1,256]{1,0:T(1,128)S(1)} %copy-done.7, s32[1,256]{1,0:T(1,128)S(1)} %copy-done.8, bf16[64,1024]{1,0:T(8,128)(2,1)S(1)} %copy-done.3, bf16[64,1024]{1,0:T(8,128)(2,1)S(1)} %copy-done.4, ...), custom_call_target="tpu_custom_call" | custom-call | tf_op jit(solution)/shard_map/encoder_block/pallas_call | solution.py:457
  150.0 0.8 copy.11
Async XLA Ops:
  0.0 0.7 copy-start.7
  0.0 0.7 copy-start.8
  0.0 0.7 copy-start.6
  0.7 1.1 copy-start
  1.8 1.0 copy-start.1
  2.9 0.9 copy-start.2
  3.8 0.9 copy-start.3
  4.7 0.9 copy-start.4
  5.6 0.7 copy-start.5

commit v3 on v2

--- a/solution.py
+++ b/solution.py
@@ -28,16 +28,23 @@
 def block_kernel(
     ring,
     shards,
+    patches_in,
+    labels_at,
+    rows_at,
+    cols_at,
+    row_table_in,
+    col_table_in,
+    gain_in,
+    w_in,
+    ow_in,
+    out,
     patches,
     labels,
     patch_rows,
     patch_cols,
-    row_table,
-    col_table,
+    table,
     gain,
-    w_own,
-    ow_own,
-    out,
+    loaded,
     w_all,
     ow_all,
     onehots,
@@ -65,12 +72,12 @@
     c_come,
     l_sent,
     l_come,
-    below_here,
-    here,
+    row_here,
+    pair_here,
 ):
     tokens, width = patches.shape
     half_tokens = tokens // 2
-    depth = w_own.shape[0]
+    depth = w_in.shape[0]
     pairs = width // LANES
     chips = shards // 2
     me = lax.axis_index("ctx")
@@ -82,41 +89,85 @@
     def mate(k, which):
         return 2 * lax.rem(chip + k, chips) + which
 
+    def columns(tile):
+        return pl.ds(pl.multiple_of(tile * LANES, LANES), LANES)
+
+    def w_rows(source):
+        return pl.ds(pl.multiple_of(source * depth, depth), depth)
+
+    def ow_place(source):
+        return ow_all.at[:, columns(source)]
+
+    grid_size = row_table_in.shape[0]
+    loads = [
+        pltpu.make_async_copy(source, target, loaded.at[k])
+        for k, (source, target) in enumerate(
+            (
+                (w_in, w_all.at[w_rows(shard), :]),
+                (rows_at, patch_rows),
+                (cols_at, patch_cols),
+                (row_table_in, table.at[pl.ds(0, grid_size), :]),
+                (col_table_in, table.at[pl.ds(grid_size, grid_size), :]),
+                (patches_in, patches),
+                (gain_in, gain),
+                (labels_at, labels),
+                (ow_in, ow_place(shard)),
+            )
+        )
+    ]
+    for load in loads:
+        load.start()
+
     barrier = pltpu.get_barrier_semaphore()
-    has_below, has_above = me > 0, me < ring - 1
-
-    def greet(**where):
-        pl.semaphore_signal(barrier, inc=1, device_id=where, device_id_type=MESH)
-
-    for k in range(1, chips):
-        greet(fsdp=mate(k, core))
-    greet(fsdp=partner)
-
-    @pl.when(has_below)
+
+    def signal(semaphore, **where):
+        pl.semaphore_signal(semaphore, inc=1, device_id=where, device_id_type=MESH)
+
+    @pl.when(shard == 0)
     def _():
-        greet(ctx=me - 1)
-
-    @pl.when(has_above)
+        pl.semaphore_wait(barrier, shards - 1)
+        for other in range(1, shards):
+            signal(row_here, fsdp=other)
+
+    @pl.when(shard > 0)
     def _():
-        greet(ctx=me + 1)
-
-    neighbours = jnp.where(has_below, 1, 0) + jnp.where(has_above, 1, 0)
-    pl.semaphore_wait(barrier, chips + neighbours)
+        signal(barrier, fsdp=0)
+        pl.semaphore_wait(row_here, 1)
+
+    @pl.when(shard > 0)
+    def _():
+        start = 2 * lax.rem(own_pair + pairs - shard, pairs)
+        signal(barrier, ctx=start)
+        signal(barrier, ctx=start + 1)
+
+    @pl.when(shard == shards - 1)
+    def _():
+        signal(barrier, ctx=4 * own_pair + 1 - me)
+
+    def meet(step):
+        ahead = far_first(pairs, step)
+
+        @pl.when((shard == ahead) & (shard > 0))
+        def _():
+            pl.semaphore_wait(barrier, jnp.where(shard == shards - 1, 3, 2))
+            for k in range(1, shards):
+                signal(pair_here.at[ahead], fsdp=lax.rem(shard + k, shards))
+
+    def met(step):
+        ahead = far_first(pairs, step)
+
+        @pl.when((shard != ahead) & (ahead > 0))
+        def _():
+            pl.semaphore_wait(pair_here.at[ahead], 1)
 
     lane = lax.broadcasted_iota(jnp.int32, (half_tokens, LANES), 1)
     low = lane < LANES // 2
     lane_full = lax.broadcasted_iota(jnp.int32, (tokens, LANES), 1)
     low_full = lane_full < LANES // 2
 
-    def columns(tile):
-        return pl.ds(pl.multiple_of(tile * LANES, LANES), LANES)
-
-    def w_rows(source):
-        return pl.ds(pl.multiple_of(source * depth, depth), depth)
-
     def w_send(tile, target):
         pltpu.make_async_remote_copy(
-            src_ref=w_own.at[:, columns(tile)],
+            src_ref=w_all.at[w_rows(shard), columns(tile)],
             dst_ref=w_all.at[w_rows(shard), columns(tile)],
             send_sem=w_sent.at[tile],
             recv_sem=w_come.at[tile, shard],
@@ -162,43 +213,18 @@
             for tile in tiles:
                 w_wait(tile, mate(k, 1 - core))
 
-    def rising_pair(step):
-        return jnp.where(step < own_pair, own_pair - 1 - step, step)
-
     def kv_tiles(step):
-        pair = rising_pair(step)
+        pair = pair_of(step)
         return pairs + pair, 2 * pairs + pair
 
     def q_tiles(step):
         return (pair_of(step),)
 
+    loads[0].wait()
     for step in range(2):
         spread(kv_tiles(step))
 
-    @pl.when(has_below)
-    def _():
-        pl.semaphore_wait(below_here, 1)
-
-    @pl.when(has_above)
-    def _():
-        pl.semaphore_signal(below_here, inc=1, device_id={"ctx": me + 1}, device_id_type=MESH)
-
-    def announce(target, carry):
-        @pl.when(target < me)
-        def _():
-            pl.semaphore_signal(
-                here.at[me], inc=1, device_id={"ctx": target}, device_id_type=MESH
-            )
-
-        return carry
-
-    lax.fori_loop(0, ring, announce, 0)
-
     def tell_labels(target):
-        @pl.when(target > me)
-        def _():
-            pl.semaphore_wait(here.at[target], 1)
-
         @pl.when(target != me)
         def _():
             pltpu.make_async_remote_copy(
@@ -210,20 +236,19 @@
                 device_id_type=MESH,
             ).start()
 
+    levels = lax.broadcasted_iota(jnp.int32, (LANES, tokens), 0)
+    for load in loads[1:]:
+        load.wait()
     labels_in[me] = labels[...]
-
-    levels = lax.broadcasted_iota(jnp.int32, (LANES, tokens), 0)
-    grid_size = row_table.shape[0]
     hit = (levels == patch_rows[...]) | (levels == patch_cols[...] + grid_size)
     onehots[...] = jnp.where(hit, 1.0, 0.0).T.astype(BF16)
-    table = jnp.concatenate([row_table[...], col_table[...]], axis=0)
     scale = gain[...]
     strip = 64
 
     def embed(i, carry):
         rows = pl.ds(pl.multiple_of(i * strip, strip), strip)
         value = patches[rows, :].astype(F32) + jnp.dot(
-            onehots[rows, :], table, preferred_element_type=F32
+            onehots[rows, :], table[...], preferred_element_type=F32
         )
         embedded[rows, :] = value
         average = jnp.mean(value, axis=-1, keepdims=True)
@@ -233,7 +258,6 @@
         return carry
 
     lax.fori_loop(0, tokens // strip, embed, 0)
-    w_all[w_rows(shard), :] = w_own[...]
 
     def project(tile):
         return jnp.dot(normed[...], w_all[:, columns(tile)], preferred_element_type=F32)
@@ -265,11 +289,13 @@
 
         k_tile, v_tile = kv_tiles(step)
         gather((k_tile, v_tile))
+        meet(step)
         keys = project(k_tile)
         values = project(v_tile)
-        first = 2 * rising_pair(step)
+        first = 2 * pair_of(step)
         kv_out[first] = jnp.where(low_full, keys, flip(values)).astype(BF16)
         kv_out[first + 1] = jnp.where(low_full, flip(keys), values).astype(BF16)
+        met(step)
         for target in (first, first + 1):
             tell_labels(target)
             deliver(kv_out, kv_in, kv_sent, kv_come, target)
@@ -277,9 +303,6 @@
 
     lax.fori_loop(0, pairs, kv_step, 0)
 
-    def ow_place(source):
-        return ow_all.at[:, columns(source)]
-
     def ow_wait(source):
         pltpu.make_async_copy(ow_place(source), ow_place(source), ow_come.at[source]).wait()
 
@@ -294,7 +317,7 @@
         def _():
             for k in order + [0]:
                 pltpu.make_async_remote_copy(
-                    src_ref=ow_own,
+                    src_ref=ow_place(shard),
                     dst_ref=ow_place(shard),
                     send_sem=ow_sent,
                     recv_sem=ow_come.at[shard],
@@ -325,7 +348,6 @@
             device_id={"fsdp": partner},
             device_id_type=MESH,
         ).start()
-    ow_all[:, columns(shard)] = ow_own[...]
 
     label_levels = levels - LANES // 2
 
@@ -354,7 +376,8 @@
     per_span = span // tokens
 
     def attend(i, carry):
-        source = jnp.where(i == 0, me, jnp.where(i <= me, i - 1, i))
+        offset = jnp.where(i == 0, 0, far_first(ring, i - 1))
+        source = lax.rem(me + offset, ring)
 
         @pl.when(i > 0)
         def _():
@@ -457,9 +480,16 @@
     result = pl.pallas_call(
         functools.partial(block_kernel, ring, shards),
         out_shape=jax.ShapeDtypeStruct((tokens, width), BF16),
-        in_specs=[pl.BlockSpec(memory_space=pltpu.VMEM)] * 9,
+        in_specs=[pl.BlockSpec(memory_space=pltpu.HBM)] * 9,
         out_specs=pl.BlockSpec(memory_space=pltpu.VMEM),
         scratch_shapes=[
+            pltpu.VMEM((tokens, width), BF16),
+            pltpu.VMEM((1, tokens), jnp.int32),
+            pltpu.VMEM((1, tokens), jnp.int32),
+            pltpu.VMEM((1, tokens), jnp.int32),
+            pltpu.VMEM((2 * row_table.shape[0], width), BF16),
+            pltpu.VMEM((1, width), F32),
+            dma((9,)),
             pltpu.VMEM((width, 3 * width), BF16),
             pltpu.VMEM((width, width), BF16),
             pltpu.VMEM((tokens, LANES), BF16),
@@ -488,10 +518,10 @@
             dma,
             dma((ring,)),
             pltpu.SemaphoreType.REGULAR,
-            pltpu.SemaphoreType.REGULAR((ring,)),
+            pltpu.SemaphoreType.REGULAR((pairs,)),
         ],
         compiler_params=pltpu.CompilerParams(
-            collective_id=0, has_side_effects=True, vmem_limit_bytes=36 << 20
+            collective_id=0, has_side_effects=True, vmem_limit_bytes=60 << 20
         ),
         name="encoder_block",
     )(

time: 151 us -> 138 us (0.914)
  the two profiles are of different devices: /device:TPU:33 before, /device:TPU:40 now
where the time goes in v3:
time: 138 us
  Pallas kernels  136 us (99%)
  local copies, waits for them, and re-layouts  1.87 us (1%)
    pallas_call x1, Pallas kernels, body(): pl.pallas_call(functools.partial(block_kernel, ring, shards), out_shape=j...  136 us

profile of v3, /device:TPU:40, one launch (start us, length us, event | category | flops | bytes accessed | tf_op | source)
XLA Modules:
  0.0 137.5 jit_solution(5192140175407791953)
XLA Ops:
  0.0 135.7 %encoder_block.1 = bf16[256,1024]{1,0:T(8,128)(2,1)} custom-call(bf16[256,1024]{1,0:T(8,128)(2,1)} %bitcast.4, s32[1,256]{1,0:T(1,128)} %labels_at.1, s32[1,256]{1,0:T(1,128)} %rows_at.1, s32[1,256]{1,0:T(1,128)} %cols_at.1, bf16[64,1024]{1,0:T(8,128)(2,1)} %row_table_in.1, bf16[64,1024]{1,0:T(8,128)(2,1)} %col_table_in.1, f32[1,1024]{1,0:T(1,128)} %bitcast.5, ...), custom_call_target="tpu_custom_call" | custom-call | tf_op jit(solution)/shard_map/encoder_block/pallas_call | solution.py:480
  135.7 1.9 %copy.11 = bf16[1,256,1024]{2,1,0:T(8,128)(2,1)} copy(bf16[1,256,1024]{2,1,0:T(8,128)(2,1)} %bitcast.3) | data formatting | bytes 1048576

commit v4 on v3

--- a/solution.py
+++ b/solution.py
@@ -217,8 +217,11 @@
         pair = pair_of(step)
         return pairs + pair, 2 * pairs + pair
 
+    def near_pair(step):
+        return pair_of(pairs - 1 - step)
+
     def q_tiles(step):
-        return (pair_of(step),)
+        return (near_pair(step),)
 
     loads[0].wait()
     for step in range(2):
@@ -329,7 +332,7 @@
         gather((tile,))
         queries = project(tile) * score_scale
         upper, lower = queries[:half_tokens], queries[half_tokens:]
-        first = 2 * pair_of(step)
+        first = 2 * near_pair(step)
         q_out[first] = jnp.where(low, upper, flip(lower)).astype(BF16)
         q_out[first + 1] = jnp.where(low, flip(upper), lower).astype(BF16)
         deliver(q_out, q_in, q_sent, q_come, first)
@@ -338,16 +341,17 @@
 
     lax.fori_loop(0, pairs, q_step, 0)
 
-    for k in order:
-        ow_wait(mate(k, core))
-        pltpu.make_async_remote_copy(
-            src_ref=ow_place(mate(k, core)),
-            dst_ref=ow_place(mate(k, core)),
-            send_sem=ow_sent,
-            recv_sem=ow_come.at[mate(k, core)],
-            device_id={"fsdp": partner},
-            device_id_type=MESH,
-        ).start()
+    def ow_forward():
+        for k in order:
+            ow_wait(mate(k, core))
+            pltpu.make_async_remote_copy(
+                src_ref=ow_place(mate(k, core)),
+                dst_ref=ow_place(mate(k, core)),
+                send_sem=ow_sent,
+                recv_sem=ow_come.at[mate(k, core)],
+                device_id={"fsdp": partner},
+                device_id_type=MESH,
+            ).start()
 
     label_levels = levels - LANES // 2
 
@@ -371,13 +375,14 @@
 
     lax.fori_loop(0, ring, widen, 0)
 
-    span = 512
-    spans = ring * tokens // span
-    per_span = span // tokens
+    everything = ring * tokens
 
     def attend(i, carry):
-        offset = jnp.where(i == 0, 0, far_first(ring, i - 1))
-        source = lax.rem(me + offset, ring)
+        source = lax.rem(me + far_first(ring, ring - 1 - i), ring)
+
+        @pl.when(i == 1)
+        def _():
+            ow_forward()
 
         @pl.when(i > 0)
         def _():
@@ -385,32 +390,41 @@
 
         block = q_in[source].astype(F32)
         hits = label_hits(source)
-        upper = jnp.where(low, block, hits[:half_tokens])
-        lower = jnp.where(low, flip(block), hits[half_tokens:])
-        queries = jnp.concatenate([upper, lower], axis=0).astype(BF16)
-        highest = jnp.full((tokens, LANES), -jnp.inf, F32)
-        for j in range(spans):
+        halves = (
+            jnp.where(low, block, hits[:half_tokens]).astype(BF16),
+            jnp.where(low, flip(block), hits[half_tokens:]).astype(BF16),
+        )
+
+        def score(half):
             part = lax.dot_general(
-                queries,
-                k_aug[pl.ds(j * span, span), :],
+                halves[half],
+                k_aug[...],
                 (((1,), (1,)), ((), ())),
                 preferred_element_type=F32,
             )
-            scores[:, pl.ds(j * span, span)] = part
-            for t in range(span // LANES):
+            scores[pl.ds(half * half_tokens, half_tokens), :] = part
+            highest = part[:, :LANES]
+            for t in range(1, everything // LANES):
                 highest = jnp.maximum(highest, part[:, t * LANES : (t + 1) * LANES])
-        top = jnp.max(highest, axis=-1, keepdims=True)
-        sums = jnp.zeros((tokens, LANES), F32)
-        mixed = jnp.zeros((tokens, LANES), F32)
-        for j in range(spans):
-            raised = jnp.exp(scores[:, pl.ds(j * span, span)] - top)
-            for t in range(span // LANES):
+            return jnp.max(highest, axis=-1, keepdims=True)
+
+        def mix(half, top):
+            raised = jnp.exp(scores[pl.ds(half * half_tokens, half_tokens), :] - top)
+            sums = raised[:, :LANES]
+            for t in range(1, everything // LANES):
                 sums = sums + raised[:, t * LANES : (t + 1) * LANES]
-            values = kv_in[pl.ds(j * per_span, per_span)].reshape(span, LANES)
-            mixed = mixed + jnp.dot(raised.astype(BF16), values, preferred_element_type=F32)
-        mixed = mixed / jnp.sum(sums, axis=-1, keepdims=True)
-        packed = jnp.where(low, flip(mixed[:half_tokens]), mixed[half_tokens:])
-        c_out[source] = packed.astype(BF16)
+            mixed = jnp.dot(
+                raised.astype(BF16),
+                kv_in[...].reshape(everything, LANES),
+                preferred_element_type=F32,
+            )
+            return mixed / jnp.sum(sums, axis=-1, keepdims=True)
+
+        top = score(0)
+        next_top = score(1)
+        upper = mix(0, top)
+        lower = mix(1, next_top)
+        c_out[source] = jnp.where(low, flip(upper), lower).astype(BF16)
         deliver(c_out, c_in, c_sent, c_come, source)
         return carry
 

time: 138 us -> 132 us (0.957)
  the two profiles are of different devices: /device:TPU:40 before, /device:TPU:33 now
where the time goes in v4:
time: 132 us; the launch traced here: 130 us
  Pallas kernels  129 us (98%)
  local copies, waits for them, and re-layouts  1.87 us (1%)
    pallas_call x1, Pallas kernels, body(): pl.pallas_call(functools.partial(block_kernel, ring, shards), out_shape=j...  129 us

profile of v4, /device:TPU:33, one launch (start us, length us, event | category | flops | bytes accessed | tf_op | source)
XLA Modules:
  0.0 130.4 jit_solution(13005803787803394443)
XLA Ops:
  0.0 128.5 %encoder_block.1 = bf16[256,1024]{1,0:T(8,128)(2,1)} custom-call(bf16[256,1024]{1,0:T(8,128)(2,1)} %bitcast.4, s32[1,256]{1,0:T(1,128)} %labels_at.1, s32[1,256]{1,0:T(1,128)} %rows_at.1, s32[1,256]{1,0:T(1,128)} %cols_at.1, bf16[64,1024]{1,0:T(8,128)(2,1)} %row_table_in.1, bf16[64,1024]{1,0:T(8,128)(2,1)} %col_table_in.1, f32[1,1024]{1,0:T(1,128)} %bitcast.5, ...), custom_call_target="tpu_custom_call" | custom-call | tf_op jit(solution)/shard_map/encoder_block/pallas_call | solution.py:494
  128.6 1.9 %copy.11 = bf16[1,256,1024]{2,1,0:T(8,128)(2,1)} copy(bf16[1,256,1024]{2,1,0:T(8,128)(2,1)} %bitcast.3) | data formatting | bytes 1048576

commit v5 on v4

--- a/solution.py
+++ b/solution.py
@@ -61,7 +61,8 @@
     scores,
     context,
     w_sent,
-    w_come,
+    mates_come,
+    partner_come,
     ow_sent,
     ow_come,
     kv_sent,
@@ -165,67 +166,59 @@
     lane_full = lax.broadcasted_iota(jnp.int32, (tokens, LANES), 1)
     low_full = lane_full < LANES // 2
 
-    def w_send(tile, target):
-        pltpu.make_async_remote_copy(
-            src_ref=w_all.at[w_rows(shard), columns(tile)],
-            dst_ref=w_all.at[w_rows(shard), columns(tile)],
-            send_sem=w_sent.at[tile],
-            recv_sem=w_come.at[tile, shard],
-            device_id={"fsdp": target},
-            device_id_type=MESH,
-        ).start()
-
-    def w_wait(tile, source):
-        place = w_all.at[w_rows(source), columns(tile)]
-        pltpu.make_async_copy(place, place, w_come.at[tile, source]).wait()
-
-    def w_forward(tile, source):
+    def pair_of(step):
+        return lax.rem(own_pair + far_first(pairs, step), pairs)
+
+    def kv_tiles(step):
+        return pairs + pair_of(step), 2 * pairs + pair_of(step)
+
+    def near_then_far(count, near, step):
+        return jnp.where(
+            step < near, far_first(count, count - 1 - step), far_first(count, step - near)
+        )
+
+    def q_pair(step):
+        return lax.rem(own_pair + near_then_far(pairs, 3, step), pairs)
+
+    def q_tiles(step):
+        return (q_pair(step),)
+
+    order = [2, 1, 3] if chips == 4 else list(range(1, chips))
+
+    def w_copy(source, tile, come, target):
         place = w_all.at[w_rows(source), columns(tile)]
         pltpu.make_async_remote_copy(
             src_ref=place,
             dst_ref=place,
-            send_sem=w_sent.at[tile],
-            recv_sem=w_come.at[tile, source],
-            device_id={"fsdp": partner},
+            send_sem=w_sent,
+            recv_sem=come,
+            device_id={"fsdp": target},
             device_id_type=MESH,
         ).start()
 
-    def pair_of(step):
-        return lax.rem(own_pair + far_first(pairs, step), pairs)
-
-    order = [2, 1, 3] if chips == 4 else list(range(1, chips))
-
-    def spread(tiles):
+    def spread(number, tiles):
         for k in order:
             for tile in tiles:
-                w_send(tile, mate(k, core))
+                w_copy(shard, tile, mates_come.at[number], mate(k, core))
         for tile in tiles:
-            w_send(tile, partner)
-
-    def gather(tiles):
-        for k in order[1:] + order[:1]:
+            w_copy(shard, tile, partner_come.at[number], partner)
+
+    def w_wait(come, blocks, tiles):
+        place = w_all.at[pl.ds(0, blocks * depth), pl.ds(0, len(tiles) * LANES)]
+        pltpu.make_async_copy(place, place, come).wait()
+
+    def hand_on(number, tiles):
+        w_wait(mates_come.at[number], chips - 1, tiles)
+        for k in order:
             for tile in tiles:
-                w_wait(tile, mate(k, core))
-                w_forward(tile, mate(k, core))
-        for tile in tiles:
-            w_wait(tile, partner)
-        for k in order[1:] + order[:1]:
-            for tile in tiles:
-                w_wait(tile, mate(k, 1 - core))
-
-    def kv_tiles(step):
-        pair = pair_of(step)
-        return pairs + pair, 2 * pairs + pair
-
-    def near_pair(step):
-        return pair_of(pairs - 1 - step)
-
-    def q_tiles(step):
-        return (near_pair(step),)
+                w_copy(mate(k, core), tile, partner_come.at[number], partner)
+
+    def gather(number, tiles):
+        w_wait(partner_come.at[number], chips, tiles)
 
     loads[0].wait()
-    for step in range(2):
-        spread(kv_tiles(step))
+    for step in range(3):
+        spread(step, kv_tiles(step))
 
     def tell_labels(target):
         @pl.when(target != me)
@@ -281,18 +274,34 @@
         def _():
             incoming[me] = outgoing[target]
 
+    hand_on(0, kv_tiles(0))
+    meet(0)
+
     def kv_step(step, carry):
-        @pl.when(step < pairs - 2)
-        def _():
-            spread(kv_tiles(step + 2))
-
-        @pl.when(step >= pairs - 2)
-        def _():
-            spread(q_tiles(step + 2 - pairs))
+        @pl.when(step < pairs - 3)
+        def _():
+            spread(step + 3, kv_tiles(step + 3))
+
+        @pl.when(step >= pairs - 3)
+        def _():
+            spread(step + 3, q_tiles(step + 3 - pairs))
+
+        def next_on():
+            @pl.when(step < pairs - 1)
+            def _():
+                hand_on(step + 1, kv_tiles(step + 1))
+
+            @pl.when(step == pairs - 1)
+            def _():
+                hand_on(pairs, q_tiles(0))
 
         k_tile, v_tile = kv_tiles(step)
-        gather((k_tile, v_tile))
-        meet(step)
+        gather(step, (k_tile, v_tile))
+
+        @pl.when(step > 0)
+        def _():
+            next_on()
+
         keys = project(k_tile)
         values = project(v_tile)
         first = 2 * pair_of(step)
@@ -302,6 +311,15 @@
         for target in (first, first + 1):
             tell_labels(target)
             deliver(kv_out, kv_in, kv_sent, kv_come, target)
+
+        @pl.when(step == 0)
+        def _():
+            next_on()
+
+        @pl.when(step < pairs - 1)
+        def _():
+            meet(step + 1)
+
         return carry
 
     lax.fori_loop(0, pairs, kv_step, 0)
@@ -312,11 +330,11 @@
     score_scale = 1.0 / (LANES // 2) ** 0.5
 
     def q_step(step, carry):
-        @pl.when(step < pairs - 2)
-        def _():
-            spread(q_tiles(step + 2))
-
-        @pl.when(step == pairs - 2)
+        @pl.when(step < pairs - 3)
+        def _():
+            spread(pairs + step + 3, q_tiles(step + 3))
+
+        @pl.when(step == pairs - 3)
         def _():
             for k in order + [0]:
                 pltpu.make_async_remote_copy(
@@ -329,10 +347,15 @@
                 ).start()
 
         (tile,) = q_tiles(step)
-        gather((tile,))
+        gather(pairs + step, (tile,))
+
+        @pl.when(step < pairs - 1)
+        def _():
+            hand_on(pairs + step + 1, q_tiles(step + 1))
+
         queries = project(tile) * score_scale
         upper, lower = queries[:half_tokens], queries[half_tokens:]
-        first = 2 * near_pair(step)
+        first = 2 * q_pair(step)
         q_out[first] = jnp.where(low, upper, flip(lower)).astype(BF16)
         q_out[first + 1] = jnp.where(low, flip(upper), lower).astype(BF16)
         deliver(q_out, q_in, q_sent, q_come, first)
@@ -378,7 +401,7 @@
     everything = ring * tokens
 
     def attend(i, carry):
-        source = lax.rem(me + far_first(ring, ring - 1 - i), ring)
+        source = lax.rem(me + near_then_far(ring, 5, i), ring)
 
         @pl.when(i == 1)
         def _():
@@ -462,12 +485,8 @@
 
     lax.fori_loop(0, width // wide, finish, 0)
 
-    def drain(tile, carry):
-        place = w_all.at[pl.ds(0, (2 * chips - 1) * depth), columns(tile)]
-        pltpu.make_async_copy(place, place, w_sent.at[tile]).wait()
-        return carry
-
-    lax.fori_loop(0, 3 * pairs, drain, 0)
+    place = w_all.at[pl.ds(0, (2 * chips - 1) * depth), :]
+    pltpu.make_async_copy(place, place, w_sent).wait()
     place = ow_all.at[:, pl.ds(0, (2 * chips - 1) * LANES)]
     pltpu.make_async_copy(place, place, ow_sent).wait()
     for buffer, sent in ((kv_out, kv_sent), (q_out, q_sent), (c_out, c_sent), (labels_in, l_sent)):
@@ -519,8 +538,9 @@
             pltpu.VMEM((ring * tokens, LANES), BF16),
             pltpu.VMEM((tokens, ring * tokens), F32),
             pltpu.VMEM((tokens, width), BF16),
-            dma((3 * pairs,)),
-            dma((3 * pairs, shards)),
+            dma,
+            dma((2 * pairs,)),
+            dma((2 * pairs,)),
             dma,
             dma((shards,)),
             dma,

time: 132 us -> 132 us (level)
  no operation moved by 1% of the time
where the time goes in v5:
time: 132 us; the launch traced here: 130 us
  Pallas kernels  129 us (98%)
  local copies, waits for them, and re-layouts  1.87 us (1%)
    pallas_call x1, Pallas kernels, body(): pl.pallas_call(functools.partial(block_kernel, ring, shards), out_shape=j...  129 us

profile of v5, /device:TPU:33, one launch (start us, length us, event | category | flops | bytes accessed | tf_op | source)
XLA Modules:
  0.0 130.5 jit_solution(9192183021200310752)
XLA Ops:
  0.0 128.6 %encoder_block.1 = bf16[256,1024]{1,0:T(8,128)(2,1)} custom-call(bf16[256,1024]{1,0:T(8,128)(2,1)} %bitcast.4, s32[1,256]{1,0:T(1,128)} %labels_at.1, s32[1,256]{1,0:T(1,128)} %rows_at.1, s32[1,256]{1,0:T(1,128)} %cols_at.1, bf16[64,1024]{1,0:T(8,128)(2,1)} %row_table_in.1, bf16[64,1024]{1,0:T(8,128)(2,1)} %col_table_in.1, f32[1,1024]{1,0:T(1,128)} %bitcast.5, ...), custom_call_target="tpu_custom_call" | custom-call | tf_op jit(solution)/shard_map/encoder_block/pallas_call | solution.py:513
  128.6 1.9 %copy.11 = bf16[1,256,1024]{2,1,0:T(8,128)(2,1)} copy(bf16[1,256,1024]{2,1,0:T(8,128)(2,1)} %bitcast.3) | data formatting | bytes 1048576

commit v6 on v5

--- a/solution.py
+++ b/solution.py
@@ -59,7 +59,6 @@
     labels_in,
     k_aug,
     scores,
-    context,
     w_sent,
     mates_come,
     partner_come,
@@ -145,8 +144,11 @@
     def _():
         signal(barrier, ctx=4 * own_pair + 1 - me)
 
+    def kv_ahead(step):
+        return far_first(pairs, jnp.where(step < 2, 1 - step, step))
+
     def meet(step):
-        ahead = far_first(pairs, step)
+        ahead = kv_ahead(step)
 
         @pl.when((shard == ahead) & (shard > 0))
         def _():
@@ -155,7 +157,7 @@
                 signal(pair_here.at[ahead], fsdp=lax.rem(shard + k, shards))
 
     def met(step):
-        ahead = far_first(pairs, step)
+        ahead = kv_ahead(step)
 
         @pl.when((shard != ahead) & (ahead > 0))
         def _():
@@ -167,7 +169,7 @@
     low_full = lane_full < LANES // 2
 
     def pair_of(step):
-        return lax.rem(own_pair + far_first(pairs, step), pairs)
+        return lax.rem(own_pair + kv_ahead(step), pairs)
 
     def kv_tiles(step):
         return pairs + pair_of(step), 2 * pairs + pair_of(step)
@@ -401,7 +403,7 @@
     everything = ring * tokens
 
     def attend(i, carry):
-        source = lax.rem(me + near_then_far(ring, 5, i), ring)
+        source = lax.rem(me + near_then_far(ring, 7, i), ring)
 
         @pl.when(i == 1)
         def _():
@@ -457,33 +459,30 @@
     for k in order:
         ow_wait(mate(k, 1 - core))
 
-    def collect(i, carry):
-        source = lax.rem(me + far_first(ring, i), ring)
-
-        @pl.when(source != me)
-        def _():
-            pltpu.make_async_copy(c_out.at[source], c_in.at[source], c_come.at[source]).wait()
-
-        return carry
-
-    lax.fori_loop(0, ring, collect, 0)
-    for pair in range(pairs):
+    wide = 256
+
+    def finish(step, carry):
+        pair = q_pair(step)
+        for head in (2 * pair, 2 * pair + 1):
+
+            @pl.when(head != me)
+            def _():
+                pltpu.make_async_copy(c_out.at[head], c_in.at[head], c_come.at[head]).wait()
+
         left = c_in[2 * pair].astype(F32)
         right = c_in[2 * pair + 1].astype(F32)
-        place = pl.ds(pair * LANES, LANES)
-        context[pl.ds(0, half_tokens), place] = jnp.where(low, left, flip(right)).astype(BF16)
-        context[pl.ds(half_tokens, half_tokens), place] = jnp.where(
-            low, flip(left), right
+        context = jnp.concatenate(
+            [jnp.where(low, left, flip(right)), jnp.where(low, flip(left), right)], axis=0
         ).astype(BF16)
-    wide = 256
-
-    def finish(i, carry):
-        place = pl.ds(pl.multiple_of(i * wide, wide), wide)
-        attended = jnp.dot(context[...], ow_all[:, place], preferred_element_type=F32)
-        out[:, place] = (embedded[:, place] + attended).astype(BF16)
+        for start in range(0, width, wide):
+            place = pl.ds(start, wide)
+            embedded[:, place] += jnp.dot(
+                context, ow_all[columns(pair), place], preferred_element_type=F32
+            )
         return carry
 
-    lax.fori_loop(0, width // wide, finish, 0)
+    lax.fori_loop(0, pairs, finish, 0)
+    out[...] = embedded[...].astype(BF16)
 
     place = w_all.at[pl.ds(0, (2 * chips - 1) * depth), :]
     pltpu.make_async_copy(place, place, w_sent).wait()
@@ -537,7 +536,6 @@
             pltpu.VMEM((ring, 1, tokens), jnp.int32),
             pltpu.VMEM((ring * tokens, LANES), BF16),
             pltpu.VMEM((tokens, ring * tokens), F32),
-            pltpu.VMEM((tokens, width), BF16),
             dma,
             dma((2 * pairs,)),
             dma((2 * pairs,)),

time: 132 us -> 131 us (level)
  no operation moved by 1% of the time
where the time goes in v6:
time: 131 us; the launch traced here: 130 us
  Pallas kernels  128 us (98%)
  local copies, waits for them, and re-layouts  1.87 us (1%)
    pallas_call x1, Pallas kernels, body(): pl.pallas_call(functools.partial(block_kernel, ring, shards), out_shape=j...  128 us

profile of v6, /device:TPU:33, one launch (start us, length us, event | category | flops | bytes accessed | tf_op | source)
XLA Modules:
  0.0 129.9 jit_solution(18010092938948144933)
XLA Ops:
  0.0 128.1 %encoder_block.1 = bf16[256,1024]{1,0:T(8,128)(2,1)} custom-call(bf16[256,1024]{1,0:T(8,128)(2,1)} %bitcast.4, s32[1,256]{1,0:T(1,128)} %labels_at.1, s32[1,256]{1,0:T(1,128)} %rows_at.1, s32[1,256]{1,0:T(1,128)} %cols_at.1, bf16[64,1024]{1,0:T(8,128)(2,1)} %row_table_in.1, bf16[64,1024]{1,0:T(8,128)(2,1)} %col_table_in.1, f32[1,1024]{1,0:T(1,128)} %bitcast.5, ...), custom_call_target="tpu_custom_call" | custom-call | tf_op jit(solution)/shard_map/encoder_block/pallas_call | solution.py:512
  128.1 1.9 %copy.11 = bf16[1,256,1024]{2,1,0:T(8,128)(2,1)} copy(bf16[1,256,1024]{2,1,0:T(8,128)(2,1)} %bitcast.3) | data formatting | bytes 1048576

commit v7 on v6

--- a/solution.py
+++ b/solution.py
@@ -48,7 +48,6 @@
     w_all,
     ow_all,
     onehots,
-    embedded,
     normed,
     kv_out,
     kv_in,
@@ -248,7 +247,7 @@
         value = patches[rows, :].astype(F32) + jnp.dot(
             onehots[rows, :], table[...], preferred_element_type=F32
         )
-        embedded[rows, :] = value
+        out[rows, :] = value
         average = jnp.mean(value, axis=-1, keepdims=True)
         centered = value - average
         variance = jnp.mean(centered * centered, axis=-1, keepdims=True)
@@ -476,13 +475,12 @@
         ).astype(BF16)
         for start in range(0, width, wide):
             place = pl.ds(start, wide)
-            embedded[:, place] += jnp.dot(
+            out[:, place] += jnp.dot(
                 context, ow_all[columns(pair), place], preferred_element_type=F32
             )
         return carry
 
     lax.fori_loop(0, pairs, finish, 0)
-    out[...] = embedded[...].astype(BF16)
 
     place = w_all.at[pl.ds(0, (2 * chips - 1) * depth), :]
     pltpu.make_async_copy(place, place, w_sent).wait()
@@ -511,7 +509,7 @@
     dma = pltpu.SemaphoreType.DMA
     result = pl.pallas_call(
         functools.partial(block_kernel, ring, shards),
-        out_shape=jax.ShapeDtypeStruct((tokens, width), BF16),
+        out_shape=jax.ShapeDtypeStruct((tokens, width), F32),
         in_specs=[pl.BlockSpec(memory_space=pltpu.HBM)] * 9,
         out_specs=pl.BlockSpec(memory_space=pltpu.VMEM),
         scratch_shapes=[
@@ -525,7 +523,6 @@
             pltpu.VMEM((width, 3 * width), BF16),
             pltpu.VMEM((width, width), BF16),
             pltpu.VMEM((tokens, LANES), BF16),
-            pltpu.VMEM((tokens, width), F32),
             pltpu.VMEM((tokens, width), BF16),
             pltpu.VMEM((ring, tokens, LANES), BF16),
             pltpu.VMEM((ring, tokens, LANES), BF16),
@@ -567,7 +564,7 @@
         qkv_weight,
         out_weight,
     )
-    return result[None]
+    return result.astype(BF16)[None]
 
 
 def solution(mesh):

time: 131 us -> 132 us (level)
  other arithmetic: 0 us -> 2.1 us
  local copies, waits for them, and re-layouts: 1.87 us -> 0 us
    broadcast_in_dim x0 -> x1, other arithmetic: none -> 2.1 us  [body(): return result.astype(BF16)[None]]
    unnamed x1 -> x0, local copies, waits for them, and re-layouts: 1.87 us -> none
where the time goes in v7:
time: 132 us; the launch traced here: 130 us
  Pallas kernels  128 us (97%)
  other arithmetic  2.1 us (2%)
    pallas_call x1, Pallas kernels, body(): pl.pallas_call(functools.partial(block_kernel, ring, shards), out_shape=j...  128 us

profile of v7, /device:TPU:33, one launch (start us, length us, event | category | flops | bytes accessed | tf_op | source)
XLA Modules:
  0.0 130.3 jit_solution(3955596902940895280)
XLA Ops:
  0.0 128.2 %encoder_block.1 = f32[256,1024]{1,0:T(8,128)} custom-call(bf16[256,1024]{1,0:T(8,128)(2,1)} %bitcast.4, s32[1,256]{1,0:T(1,128)} %labels_at.1, s32[1,256]{1,0:T(1,128)} %rows_at.1, s32[1,256]{1,0:T(1,128)} %cols_at.1, bf16[64,1024]{1,0:T(8,128)(2,1)} %row_table_in.1, bf16[64,1024]{1,0:T(8,128)(2,1)} %col_table_in.1, f32[1,1024]{1,0:T(1,128)} %bitcast.5, ...), custom_call_target="tpu_custom_call" | custom-call | tf_op jit(solution)/shard_map/encoder_block/pallas_call | solution.py:510
  128.2 2.1 %convert_bitcast_fusion = bf16[1,256,1024]{2,1,0:T(8,128)(2,1)} fusion(f32[256,1024]{1,0:T(8,128)} %encoder_block.1), kind=kLoop, calls=%fused_computation | loop fusion | flops 262144 | bytes 1572864 | tf_op jit(solution)/shard_map/broadcast_in_dim | solution.py:567
